TPU v7x, 32 devices: a whole 2x2x4 slice. The times are simulated.
32 devices in a mesh: section: 2 (over core), shard: 4 (over z), rep: 4 (over y, x).
Axes of the slice: x: 2, y: 2, z: 4, core: 2. Of those that a mesh axis runs over, the one named last changes fastest.
Arguments:
- boundary: bfloat16 [2, 2, 16, 256, 1536], P('section', None, ('shard', 'rep')), may hold values from -6 to 6
- lengths: int32 [2, 16], P(None, ('shard', 'rep')), may hold values from 1 to 256, 2457 in all within a row
- in_proj: bfloat16 [2, 1536, 6400], P('section', 'shard'), may hold values from -0.15625 to 0.15625
- dt_proj: bfloat16 [2, 1536, 48], P('section', 'shard'), may hold values from -0.15625 to 0.15625
- out_proj: bfloat16 [2, 3072, 1536], P('section', 'shard'), may hold values from -0.109375 to 0.109375
- conv_weight: bfloat16 [2, 4, 3328], P('section', None, 'shard'), may hold values from -3 to 3
- conv_bias: bfloat16 [2, 3328], P('section', 'shard'), may hold values from -3 to 3
- dt_bias: bfloat16 [2, 48], P('section', 'shard'), may hold values from -6 to -2
- a_log: bfloat16 [2, 48], P('section', 'shard'), may hold values from 0 to 2.765625
- d_skip: bfloat16 [2, 48], P('section', 'shard'), may hold values from 0.5 to 1.5
- pre_gain: bfloat16 [2, 1536], P('section', 'shard'), may hold values from 0.5 to 1.5
- out_gain: bfloat16 [2, 3072], P('section', 'shard'), may hold values from 0.5 to 1.5
Outputs:
- activations: bfloat16 [2, 2, 16, 256, 1536], P('section', None, ('shard', 'rep'))
- input_grads: bfloat16 [2, 2, 16, 256, 1536], P('section', None, ('shard', 'rep'))
- grad_in_proj: float32 [2, 1536, 6400], P('section', 'shard')
- grad_dt_proj: float32 [2, 1536, 48], P('section', 'shard')
- grad_out_proj: float32 [2, 3072, 1536], P('section', 'shard')
- grad_conv_weight: float32 [2, 4, 3328], P('section', None, 'shard')
- grad_conv_bias: float32 [2, 3328], P('section', 'shard')
- grad_dt_bias: float32 [2, 48], P('section', 'shard')
- grad_a_log: float32 [2, 48], P('section', 'shard')
- grad_d_skip: float32 [2, 48], P('section', 'shard')
- grad_pre_gain: float32 [2, 1536], P('section', 'shard')
- grad_out_gain: float32 [2, 3072], P('section', 'shard')
Inputs may be any that keep to these rules, and one draw needn't show every extreme that they name: `lengths`: in each micro-batch some sequence has exactly 256 tokens.
All inputs are finite; a program needn't handle non-finite values. No bound on the sum of `lengths` on one device may be relied on, other than what follows from the above.
Results may differ from a plain program's by a relative error of at most 0.02.
Values may be sent and summed in bfloat16 or wider, within the bound.
A program may use at most 768 MiB of HBM per device.

v0:
```python
import jax
import jax.numpy as jnp
from jax import lax
from jax.sharding import PartitionSpec as P

SCAN_BLOCK = 128
HIGH = lax.Precision.HIGHEST
EPSILON = 1e-05


def from_behind(value, axis, steps):
    count = lax.axis_size(axis)
    first, last = (max(0, -steps), min(count, count - steps))
    return lax.ppermute(value, axis, [(source, source + steps) for source in range(first, last)])


def as_sent(x):

    def short(part):
        return part.astype(jnp.bfloat16) if part.dtype == jnp.float32 else part

    return jax.tree.map(short, x)


def pre_norm(rows, gain_row):
    return rows * lax.rsqrt(jnp.mean(rows * rows, axis=-1, keepdims=True) + EPSILON) * gain_row


def state_space(inputs, decay, b_rows, c_rows):
    seq_len, heads, head_dim = inputs.shape
    state_dim = b_rows.shape[1]
    blocks = seq_len // SCAN_BLOCK
    x_blocks = inputs.reshape(blocks, SCAN_BLOCK, heads, head_dim)
    d_blocks = decay.reshape(blocks, SCAN_BLOCK, heads)
    b_blocks = b_rows.reshape(blocks, SCAN_BLOCK, state_dim)
    c_blocks = c_rows.reshape(blocks, SCAN_BLOCK, state_dim)
    places = jnp.arange(SCAN_BLOCK, dtype=jnp.int32)
    lower = (places[:, None] >= places[None, :])[None, :, :]

    def advance(carried, pieces):
        x_piece, d_piece, b_piece, c_piece = pieces
        cumul = jnp.cumsum(d_piece, axis=0).T
        spread = cumul[:, :, None] - cumul[:, None, :]
        weights = jnp.where(lower, jnp.exp(jnp.where(lower, spread, 0.0)), 0.0)
        scores = jnp.dot(c_piece, b_piece.T, precision=HIGH)
        inside = jnp.einsum("hij,jhp->ihp", weights * scores[None], x_piece, precision=HIGH)
        from_state = (
            jnp.einsum("in,hpn->ihp", c_piece, carried, precision=HIGH)
            * jnp.exp(cumul).T[:, :, None]
        )
        tail = jnp.exp(cumul[:, -1:] - cumul).T
        fresh = jnp.einsum("jhp,jn->hpn", x_piece * tail[:, :, None], b_piece, precision=HIGH)
        updated = jnp.exp(cumul[:, -1])[:, None, None] * carried + fresh
        return (updated, inside + from_state)

    start = jnp.zeros((heads, head_dim, state_dim), jnp.float32)
    _, outputs = lax.scan(advance, start, (x_blocks, d_blocks, b_blocks, c_blocks))
    return outputs.reshape(seq_len, heads, head_dim)


def mixer_core(projected, dt_raw, floats):
    conv_weight, conv_bias, dt_bias, a_log, d_skip, out_gain = floats
    inner = out_gain.shape[0]
    heads = dt_bias.shape[0]
    state_dim = (conv_weight.shape[1] - inner) // 2
    taps = conv_weight.shape[0]
    seq_len = projected.shape[0]
    gate_part = projected[:, :inner]
    conv_in = projected[:, inner:]
    padded = jnp.pad(conv_in, ((taps - 1, 0), (0, 0)))
    summed = conv_bias + conv_weight[0] * padded[0:seq_len]
    for offset in range(1, taps):
        summed = summed + conv_weight[offset] * padded[offset : offset + seq_len]
    conv_act = jax.nn.silu(summed)
    x_part = conv_act[:, :inner].reshape(seq_len, heads, inner // heads)
    b_rows = conv_act[:, inner : inner + state_dim]
    c_rows = conv_act[:, inner + state_dim :]
    step_size = jax.nn.softplus(dt_raw + dt_bias)
    decay = -jnp.exp(a_log) * step_size
    output = (
        state_space(x_part * step_size[:, :, None], decay, b_rows, c_rows)
        + d_skip[None, :, None] * x_part
    )
    gated = output.reshape(seq_len, inner) * jax.nn.silu(gate_part)
    return pre_norm(gated, out_gain)


def core_floats(params):
    return tuple((params[place].astype(jnp.float32) for place in (3, 4, 5, 6, 7, 9)))


def live_mask(seq_len, count):
    return (jnp.arange(seq_len, dtype=jnp.int32) < count).astype(jnp.float32)[:, None]


def block_forward(rows, count, params):
    rows32 = rows.astype(jnp.float32)
    normed = pre_norm(rows32, params[8].astype(jnp.float32)).astype(jnp.bfloat16)
    projected = jnp.dot(normed, params[0], preferred_element_type=jnp.float32)
    dt_raw = jnp.dot(normed, params[1], preferred_element_type=jnp.float32)
    mixed = mixer_core(projected, dt_raw, core_floats(params)).astype(jnp.bfloat16)
    out_rows = jnp.dot(mixed, params[2], preferred_element_type=jnp.float32)
    result = (rows32 + live_mask(rows.shape[0], count) * out_rows).astype(jnp.bfloat16)
    return (result, (normed, projected, dt_raw, mixed))


def block_backward(cotangent, rows, stored, count, params):
    normed, projected, dt_raw, mixed = stored
    cot32 = cotangent.astype(jnp.float32)
    g_out = (cot32 * live_mask(rows.shape[0], count)).astype(jnp.bfloat16)
    d_out_proj = jnp.einsum("lk,ld->kd", mixed, g_out, preferred_element_type=jnp.float32)
    d_mixed = jnp.einsum("ld,kd->lk", g_out, params[2], preferred_element_type=jnp.float32)
    _, core_back = jax.vjp(mixer_core, projected, dt_raw, core_floats(params))
    d_projected, d_dt_raw, d_floats = core_back(d_mixed)
    d_proj_low = d_projected.astype(jnp.bfloat16)
    d_dt_low = d_dt_raw.astype(jnp.bfloat16)
    d_in_proj = jnp.einsum("ld,lk->dk", normed, d_proj_low, preferred_element_type=jnp.float32)
    d_dt_proj = jnp.einsum("ld,lk->dk", normed, d_dt_low, preferred_element_type=jnp.float32)
    d_normed = jnp.einsum(
        "lk,dk->ld", d_proj_low, params[0], preferred_element_type=jnp.float32
    ) + jnp.einsum("lk,dk->ld", d_dt_low, params[1], preferred_element_type=jnp.float32)
    _, norm_back = jax.vjp(pre_norm, rows.astype(jnp.float32), params[8].astype(jnp.float32))
    d_rows, d_pre_gain = norm_back(d_normed)
    d_input = (cot32 + d_rows).astype(jnp.bfloat16)
    grads = (
        d_in_proj,
        d_dt_proj,
        d_out_proj,
        d_floats[0],
        d_floats[1],
        d_floats[2],
        d_floats[3],
        d_floats[4],
        d_pre_gain,
        d_floats[5],
    )
    return (d_input, grads)


def add_trees(left, right):
    return tuple((a + b for a, b in zip(left, right)))


def on_device(
    boundary,
    lengths,
    in_proj,
    dt_proj,
    out_proj,
    conv_weight,
    conv_bias,
    dt_bias,
    a_log,
    d_skip,
    pre_gain,
    out_gain,
):
    section_index = lax.axis_index("section")
    shards = (
        in_proj,
        dt_proj,
        out_proj,
        conv_weight,
        conv_bias,
        dt_bias,
        a_log,
        d_skip,
        pre_gain,
        out_gain,
    )
    gathered = (
        lax.all_gather(shards[0], "shard", axis=1, tiled=True),
        lax.all_gather(shards[1], "shard", axis=1, tiled=True),
        lax.all_gather(shards[2], "shard", axis=1, tiled=True),
        lax.all_gather(shards[3], "shard", axis=2, tiled=True),
        lax.all_gather(shards[4], "shard", axis=1, tiled=True),
        lax.all_gather(shards[5], "shard", axis=1, tiled=True),
        lax.all_gather(shards[6], "shard", axis=1, tiled=True),
        lax.all_gather(shards[7], "shard", axis=1, tiled=True),
        lax.all_gather(shards[8], "shard", axis=1, tiled=True),
        lax.all_gather(shards[9], "shard", axis=1, tiled=True),
    )
    params = tuple((item[0] for item in gathered))
    own_rows = boundary[0, :, 0]
    own_counts = lengths[:, 0]
    micro = own_rows.shape[0]
    seq_len = own_rows.shape[1]
    width = own_rows.shape[2]

    def zero_stored():
        return (
            jnp.zeros((seq_len, width), jnp.bfloat16),
            jnp.zeros((seq_len, params[0].shape[1]), jnp.float32),
            jnp.zeros((seq_len, params[1].shape[1]), jnp.float32),
            jnp.zeros((seq_len, params[2].shape[0]), jnp.bfloat16),
        )

    def run_forward(rows, count):
        return block_forward(rows, count, params)

    def spare_forward(rows, count):
        return (jnp.zeros((seq_len, width), jnp.bfloat16), zero_stored())

    incoming = jnp.zeros((seq_len, width), jnp.bfloat16)
    outputs = jnp.zeros((micro, seq_len, width), jnp.bfloat16)
    saved = []
    for moment in range(micro + 1):
        micro_index = moment - section_index
        active = (micro_index >= 0) & (micro_index < micro)
        slot_index = jnp.clip(micro_index, 0, micro - 1)
        block_in = jnp.where(
            section_index == 0, lax.dynamic_index_in_dim(own_rows, slot_index, 0, False), incoming
        )
        count = lax.dynamic_index_in_dim(own_counts, slot_index, 0, False)
        result, stored = lax.cond(active, run_forward, spare_forward, block_in, count)
        outputs = jnp.where(
            active, lax.dynamic_update_index_in_dim(outputs, result, slot_index, 0), outputs
        )
        saved.append((block_in, stored, count, active, slot_index))
        if moment < micro:
            incoming = from_behind(result, "section", 1)
    regathered = (
        lax.all_gather(shards[0], "shard", axis=1, tiled=True),
        lax.all_gather(shards[1], "shard", axis=1, tiled=True),
        lax.all_gather(shards[2], "shard", axis=1, tiled=True),
        lax.all_gather(shards[3], "shard", axis=2, tiled=True),
        lax.all_gather(shards[4], "shard", axis=1, tiled=True),
        lax.all_gather(shards[5], "shard", axis=1, tiled=True),
        lax.all_gather(shards[6], "shard", axis=1, tiled=True),
        lax.all_gather(shards[7], "shard", axis=1, tiled=True),
        lax.all_gather(shards[8], "shard", axis=1, tiled=True),
        lax.all_gather(shards[9], "shard", axis=1, tiled=True),
    )
    back_params = tuple((item[0] for item in regathered))

    def run_backward(cotangent, rows, stored, count):
        return block_backward(cotangent, rows, stored, count, back_params)

    def spare_backward(cotangent, rows, stored, count):
        return (
            jnp.zeros((seq_len, width), jnp.bfloat16),
            tuple((jnp.zeros(item.shape, jnp.float32) for item in back_params)),
        )

    incoming_grad = jnp.zeros((seq_len, width), jnp.bfloat16)
    in_grads = jnp.zeros((micro, seq_len, width), jnp.bfloat16)
    total = None
    for moment in range(micro + 1):
        block_in, stored, count, active, slot_index = saved[micro - moment]
        cotangent = jnp.where(
            section_index == 1,
            lax.dynamic_index_in_dim(own_rows, slot_index, 0, False),
            incoming_grad,
        )
        d_input, grads = lax.cond(
            active, run_backward, spare_backward, cotangent, block_in, stored, count
        )
        in_grads = jnp.where(
            active, lax.dynamic_update_index_in_dim(in_grads, d_input, slot_index, 0), in_grads
        )
        if moment < micro:
            incoming_grad = from_behind(d_input, "section", -1)
        total = grads if total is None else add_trees(total, grads)
    owned = (
        lax.psum_scatter(
            total[0].astype(jnp.bfloat16), "shard", scatter_dimension=0, tiled=True
        ).astype(jnp.float32),
        lax.psum_scatter(
            total[1].astype(jnp.bfloat16), "shard", scatter_dimension=0, tiled=True
        ).astype(jnp.float32),
        lax.psum_scatter(
            total[2].astype(jnp.bfloat16), "shard", scatter_dimension=0, tiled=True
        ).astype(jnp.float32),
        lax.psum_scatter(
            total[3].astype(jnp.bfloat16), "shard", scatter_dimension=1, tiled=True
        ).astype(jnp.float32),
        lax.psum_scatter(
            total[4].astype(jnp.bfloat16), "shard", scatter_dimension=0, tiled=True
        ).astype(jnp.float32),
        lax.psum_scatter(
            total[5].astype(jnp.bfloat16), "shard", scatter_dimension=0, tiled=True
        ).astype(jnp.float32),
        lax.psum_scatter(
            total[6].astype(jnp.bfloat16), "shard", scatter_dimension=0, tiled=True
        ).astype(jnp.float32),
        lax.psum_scatter(
            total[7].astype(jnp.bfloat16), "shard", scatter_dimension=0, tiled=True
        ).astype(jnp.float32),
        lax.psum_scatter(
            total[8].astype(jnp.bfloat16), "shard", scatter_dimension=0, tiled=True
        ).astype(jnp.float32),
        lax.psum_scatter(
            total[9].astype(jnp.bfloat16), "shard", scatter_dimension=0, tiled=True
        ).astype(jnp.float32),
    )
    summed = jax.tree.map(lambda part: part.astype(jnp.float32), lax.psum(as_sent(owned), "rep"))
    final = tuple((item[None] for item in summed))
    return (
        outputs[None, :, None],
        in_grads[None, :, None],
        final[0],
        final[1],
        final[2],
        final[3],
        final[4],
        final[5],
        final[6],
        final[7],
        final[8],
        final[9],
    )


def solution(mesh):
    in_specs = (
        P("section", None, ("shard", "rep"), None, None),
        P(None, ("shard", "rep")),
        P("section", "shard", None),
        P("section", "shard", None),
        P("section", "shard", None),
        P("section", None, "shard"),
        P("section", "shard"),
        P("section", "shard"),
        P("section", "shard"),
        P("section", "shard"),
        P("section", "shard"),
        P("section", "shard"),
    )
    out_specs = (
        P("section", None, ("shard", "rep"), None, None),
        P("section", None, ("shard", "rep"), None, None),
        P("section", "shard", None),
        P("section", "shard", None),
        P("section", "shard", None),
        P("section", None, "shard"),
        P("section", "shard"),
        P("section", "shard"),
        P("section", "shard"),
        P("section", "shard"),
        P("section", "shard"),
        P("section", "shard"),
    )
    return jax.shard_map(
        on_device, mesh=mesh, in_specs=in_specs, out_specs=out_specs, check_vma=False
    )
```

profile of v0, /device:TPU:0, one launch (start us, length us, event | category | flops | bytes accessed | tf_op | source)
XLA Modules:
  0.0 2693.9 jit_solution(14970451352565655027)
XLA Ops:
  12.0 57.2 %all_gather.41 = bf16[1,4,3328]{1,0,2:T(2,128)(2,1)S(1)} all-gather(bf16[1,4,832]{1,0,2:T(2,128)(2,1)} %copy.733), channel_id=1, replica_groups=mesh['section'=2,'shard'=4,'rep'=4] {'shard'}, dimensions={2}, use_global_device_ids=true | all-gather | bytes 33280 | tf_op jit(solution)/shard_map/all_gather | solution.py:175
  71.0 18.8 all_gather.48
  89.9 14.1 all_gather.42
  118.8 26.5 all_gather.44
  146.3 59.6 %all-gather.5.cloned.1.call-done = bf16[1,3072,1536]{2,1,0:T(8,128)(2,1)} async-done(((bf16[1,768,1536]{2,1,0:T(8,128)(2,1)}), bf16[1,3072,1536]{2,1,0:T(8,128)(2,1)}) %all-gather.5.cloned.1.call-update) | async-done | bytes 9437200 | tf_op jit(solution)/shard_map/all_gather | solution.py:174
  205.8 336.6 %all-gather.3.cloned.1.call-done = bf16[1,1536,6400]{2,1,0:T(8,128)(2,1)} async-done(((bf16[1,384,6400]{2,1,0:T(8,128)(2,1)}), bf16[1,1536,6400]{2,1,0:T(8,128)(2,1)}) %all-gather.3.cloned.1.call-update) | async-done | bytes 19660816 | tf_op jit(solution)/shard_map/all_gather | solution.py:172
  542.4 112.4 %conditional.6 = (bf16[256,1536]{1,0:T(8,128)(2,1)}, bf16[256,1536]{1,0:T(8,128)(2,1)}, f32[256,6400]{1,0:T(8,128)}, f32[256,48]{0,1:T(8,128)}, bf16[256,3072]{1...) conditional(s32[]{:T(128)} %convert_element_type.338, () %tuple.200, (bf16[256,1536]{1,0:T(8,128)(2,1)S(1)}, s32[]{:T(128)}, ...), branch_computations={%region_0.1_spmd, %region_1.7_spmd} | conditional | flops 9355532288 | bytes 165452624 | solution.py:215
  583.5 43.0 %while.240 = (s32[]{:T(128)}, f32[48,64,128]{2,1,0:T(8,128)S(1)}, f32[2,128,48,64]{1,3,2,0:T(8,128)}, f32[2,128,48]{2,1,0:T(8,128)S(1)}, f32[2,128,48,64]{1,0,3,...) while((s32[]{:T(128)}, f32[48,64,128]{2,1,0:T(8,128)S(1)}, ...), condition=%wide.region_5.5_spmd.clone.clone, body=%wide.region_3.4_spmd.clone.clone.sunk | while | flops 1843806208 | bytes 17469076 | solution.py:57
  661.3 113.3 %conditional.7 = (bf16[256,1536]{1,0:T(8,128)(2,1)}, bf16[256,1536]{1,0:T(8,128)(2,1)}, f32[256,6400]{1,0:T(8,128)}, f32[256,48]{0,1:T(8,128)}, bf16[256,3072]{1...) conditional(s32[]{:T(128)} %convert_element_type.339, () %tuple.202, (bf16[256,1536]{1,0:T(8,128)(2,1)S(1)}, s32[]{:T(128)}, ...), branch_computations={%region_7.8_spmd, %region_8.14_spmd} | conditional | flops 9355532288 | bytes 165452624 | solution.py:215
  703.2 43.2 %while.241 = (s32[]{:T(128)}, f32[48,64,128]{2,1,0:T(8,128)S(1)}, f32[2,128,48,64]{1,3,2,0:T(8,128)}, f32[2,128,48]{2,1,0:T(8,128)S(1)}, f32[2,128,48,64]{1,0,3,...) while((s32[]{:T(128)}, f32[48,64,128]{2,1,0:T(8,128)S(1)}, ...), condition=%wide.region_12.12_spmd.clone.clone, body=%wide.region_10.11_spmd.clone.clone.sunk | while | flops 1843806208 | bytes 17469076 | solution.py:57
  793.3 32.9 %conditional.9 = (bf16[256,1536]{1,0:T(8,128)(2,1)}, f32[1536,48]{0,1:T(8,128)}, f32[4,3328]{1,0:T(4,128)}, f32[3328]{0:T(1024)}, f32[48]{0:T(128)}, /*index=5*/...) conditional(s32[]{:T(128)} %convert_element_type.340, ...), branch_computations={%region_21.22_spmd, %region_22.0_spmd} | conditional | flops 20592838656 | bytes 814240640 | solution.py:255
  827.5 422.0 %collective-permute-done.2 = bf16[256,1536]{1,0:T(8,128)(2,1)S(1)} collective-permute-done((bf16[256,1536]{1,0:T(8,128)(2,1)}, bf16[256,1536]{1,0:T(8,128)(2,1)S(1)}, u32[]{:S(2)}, u32[]{:S(2)}) %collective-permute-start.2) | collective-permute-done | bytes 786464 | tf_op jit(solution)/shard_map/ppermute | solution.py:14
  1249.5 352.6 %conditional.10 = (bf16[256,1536]{1,0:T(8,128)(2,1)}, f32[1536,48]{0,1:T(8,128)}, f32[4,3328]{1,0:T(4,128)}, f32[3328]{0:T(1024)}, f32[48]{0:T(128)}, /*index=5*...) conditional(s32[]{:T(128)} %convert_element_type.339, ...), branch_computations={%region_52.54_spmd, %region_53.84_spmd} | conditional | flops 20592838656 | bytes 781147136 | solution.py:255
  1283.1 60.2 %while.245 = (s32[]{:T(128)}, f32[48,64,128]{2,1,0:T(8,128)S(1)}, f32[2,128,48,64]{1,3,2,0:T(8,128)}, f32[2,48,128,128]{3,2,1,0:T(8,128)}, f32[2,128,128]{1,2,0:...) while((s32[]{:T(128)}, f32[48,64,128]{2,1,0:T(8,128)S(1)}, ...), condition=%wide.region_56.57_spmd.clone.clone, body=%wide.region_54.56_spmd.clone.clone.sunk | while | flops 1847734272 | bytes 84601144 | solution.py:57
  1389.8 68.0 %while.246 = (s32[]{:T(128)}, f32[48,64,128]{2,1,0:T(8,128)S(1)}, f32[2,128,48,64]{1,3,2,0:T(8,128)}, f32[2,128,48]{2,1,0:T(8,128)S(1)}, f32[2,128,128]{2,1,0:T(...) while((s32[]{:T(128)}, f32[48,64,128]{2,1,0:T(8,128)S(1)}, ...), condition=%wide.region_68.69_spmd.clone.clone, body=%wide.region_59.68_spmd.clone.clone.sunk | while | flops 3687632896 | bytes 91598432 | solution.py:57
  1489.6 17.5 convolution_bitcast_fusion.3
  1507.1 39.4 %copy.772 = f32[1536,6400]{1,0:T(8,128)} copy(f32[1536,6400]{0,1:T(8,128)} %convolution_bitcast_fusion.3) | data formatting | bytes 78643200 | tf_op jit(solution)/shard_map/cond | solution.py:255
  1583.4 18.7 copy.774
  1606.5 350.7 %conditional.11 = (f32[1536,48]{0,1:T(8,128)}, f32[4,3328]{1,0:T(4,128)}, f32[3328]{0:T(1024)}, f32[48]{0:T(128)}, f32[48]{0:T(128)}, /*index=5*/f32[48]{0:T(128...) conditional(s32[]{:T(128)} %convert_element_type.338, ...), branch_computations={%region_83.85_spmd, %region_84.115_spmd} | conditional | flops 20592838656 | bytes 793205952 | solution.py:255
  1640.2 60.4 %while.247 = (s32[]{:T(128)}, f32[48,64,128]{2,1,0:T(8,128)S(1)}, f32[2,128,48,64]{1,3,2,0:T(8,128)}, f32[2,48,128,128]{3,2,1,0:T(8,128)}, f32[2,128,128]{1,2,0:...) while((s32[]{:T(128)}, f32[48,64,128]{2,1,0:T(8,128)S(1)}, ...), condition=%wide.region_87.88_spmd.clone.clone, body=%wide.region_85.87_spmd.clone.clone.sunk | while | flops 1847734272 | bytes 84601144 | solution.py:57
  1747.5 68.0 %while.248 = (s32[]{:T(128)}, f32[48,64,128]{2,1,0:T(8,128)S(1)}, f32[2,128,48,64]{1,3,2,0:T(8,128)}, f32[2,128,48]{2,1,0:T(8,128)S(1)}, f32[2,128,128]{2,1,0:T(...) while((s32[]{:T(128)}, f32[48,64,128]{2,1,0:T(8,128)S(1)}, ...), condition=%wide.region_99.100_spmd.clone.clone, body=%wide.region_90.99_spmd.clone.clone.sunk | while | flops 3687632896 | bytes 91598432 | solution.py:57
  1847.0 17.4 convolution_bitcast_fusion.6
  1864.4 39.6 %copy.776 = f32[1536,6400]{1,0:T(8,128)} copy(f32[1536,6400]{0,1:T(8,128)} %convolution_bitcast_fusion.6) | data formatting | bytes 78643200 | tf_op jit(solution)/shard_map/cond | solution.py:255
  1938.4 18.6 copy.778
  1957.2 22.4 add_convert_fusion.10
  1979.7 44.0 %add_convert_fusion.9 = bf16[1536,6400]{1,0:T(8,128)(2,1)} fusion(f32[1536,6400]{1,0:T(8,128)} %get-tuple-element.5079, f32[1536,6400]{1,0:T(8,128)} %get-tuple-element.5075, f32[1536,6400]{1,0:T(8,128)} %get-tuple-element.5077), kind=kLoop, calls=%fused_computation.929 | loop fusion | flops 29491200 | bytes 137625600 | tf_op jit(solution)/shard_map/convert_element_type | solution.py:266
  2028.2 111.5 %reduce-scatter.11.cloned.1.call-done = bf16[768,1536]{1,0:T(8,128)(2,1)} async-done(((bf16[3072,1536]{1,0:T(8,128)(2,1)}), bf16[768,1536]{1,0:T(8,128)(2,1)}) %reduce-scatter.11.cloned.1.call-update) | async-done | bytes 2359312 | tf_op jit(solution)/shard_map/reduce_scatter | solution.py:271
  2139.7 329.7 %reduce-scatter.9.cloned.1.call-done = bf16[384,6400]{1,0:T(8,128)(2,1)} async-done(((bf16[1536,6400]{1,0:T(8,128)(2,1)}), bf16[384,6400]{1,0:T(8,128)(2,1)}) %reduce-scatter.9.cloned.1.call-update) | async-done | bytes 4915216 | tf_op jit(solution)/shard_map/reduce_scatter | solution.py:265
  2481.3 19.3 all-reduce.63
  2503.8 16.3 reduce-scatter.13.cloned.1.call-done
  2521.1 18.2 all-reduce.61
  2543.8 133.1 %all-reduce.67.cloned.1.call-done = (bf16[1,384,6400]{2,1,0:T(8,128)(2,1)}, bf16[1,768,1536]{2,1,0:T(8,128)(2,1)}) async-done(((bf16[1,384,6400]{2,1,0:T(8,128)(2,1)}, bf16[1,768,1536]{2,1,0:T(8,128)(2,1)}), (bf16[1,384,6400]{2,1,0:T(8,128)(2,1)}, bf16[1,768,1536]{2,1,0:T(8,128)(2,1)})) %all-reduce.67.cloned.1.call-update) | async-done | bytes 7274512 | tf_op jit(solution)/shard_map/psum | solution.py:296
  (1128 shorter events, 887.5 us)
Async XLA Ops:
  7.2 198.6 %all-gather.5.cloned.1.call-start = ((), (), s32[]{:S(2)}) async-start(), calls=%async_computation.5 | async-start | bytes 11796480 | tf_op jit(solution)/shard_map/all_gather | solution.py:174
  7.9 534.5 %all-gather.3.cloned.1.call-start = ((), (), s32[]{:S(2)}) async-start(), calls=%async_computation.4 | async-start | bytes 24576000 | tf_op jit(solution)/shard_map/all_gather | solution.py:172
  8.7 62.1 %copy-start.253 = (bf16[1,384,48]{1,2,0:T(8,128)(2,1)S(1)}, bf16[1,384,48]{1,2,0:T(8,128)(2,1)}, u32[]{:S(2)}) copy-start(bf16[1,384,48]{1,2,0:T(8,128)(2,1)} %param.46) | copy-start | bytes 110596
  8.7 62.2 %copy-start.277 = (bf16[1,832]{1,0:T(2,128)(2,1)S(1)}, bf16[1,832]{1,0:T(2,128)(2,1)}, u32[]{:S(2)}) copy-start(bf16[1,832]{1,0:T(2,128)(2,1)} %param.49) | copy-start | bytes 4996
  8.7 62.3 %copy-start.278 = (bf16[1,768]{1,0:T(2,128)(2,1)S(1)}, bf16[1,768]{1,0:T(2,128)(2,1)}, u32[]{:S(2)}) copy-start(bf16[1,768]{1,0:T(2,128)(2,1)} %param.54) | copy-start | bytes 4612
  8.7 81.1 %copy-start.292 = (bf16[1,384]{1,0:T(2,128)(2,1)S(1)}, bf16[1,384]{1,0:T(2,128)(2,1)}, u32[]{:S(2)}) copy-start(bf16[1,384]{1,0:T(2,128)(2,1)} %param.53) | copy-start | bytes 2308
  8.7 95.3 %copy-start.293 = (bf16[1,12]{1,0:T(2,128)(2,1)S(1)}, bf16[1,12]{1,0:T(2,128)(2,1)}, u32[]{:S(2)}) copy-start(bf16[1,12]{1,0:T(2,128)(2,1)} %param.51) | copy-start | bytes 76
  8.7 95.6 %copy-start.294 = (bf16[1,12]{1,0:T(2,128)(2,1)S(1)}, bf16[1,12]{1,0:T(2,128)(2,1)}, u32[]{:S(2)}) copy-start(bf16[1,12]{1,0:T(2,128)(2,1)} %param.52) | copy-start | bytes 76
  8.7 95.8 %copy-start.295 = (bf16[1,12]{1,0:T(2,128)(2,1)S(1)}, bf16[1,12]{1,0:T(2,128)(2,1)}, u32[]{:S(2)}) copy-start(bf16[1,12]{1,0:T(2,128)(2,1)} %param.50) | copy-start | bytes 76
  8.8 96.2 %copy-start.276 = (s32[2,1]{0,1:T(1,128)S(1)}, s32[2,1]{0,1:T(1,128)}, u32[]{:S(2)}) copy-start(s32[2,1]{0,1:T(1,128)} %param.44) | copy-start | bytes 28
  8.8 136.5 %copy-start.97 = (bf16[1,2,1,256,1536]{4,3,2,1,0:T(8,128)(2,1)S(1)}, bf16[1,2,1,256,1536]{4,3,2,1,0:T(8,128)(2,1)}, u32[]{:S(2)}) copy-start(bf16[1,2,1,256,1536]{4,3,2,1,0:T(8,128)(2,1)} %param.43) | copy-start | bytes 4718596
  8.8 2130.9 %reduce-scatter.11.cloned.1.call-start = ((), (), s32[]{:S(2)}) async-start(), calls=%async_computation.7 | async-start | bytes 11796480 | tf_op jit(solution)/shard_map/reduce_scatter | solution.py:271
  70.8 471.6 %copy-start.120 = (bf16[1,4,3328]{2,1,0:T(4,128)(2,1)}, bf16[1,4,3328]{2,1,0:T(4,128)(2,1)S(1)}, u32[]{:S(2)}) copy-start(bf16[1,4,3328]{2,1,0:T(4,128)(2,1)S(1)} %copy.734) | copy-start | bytes 79876
  89.9 703.4 %copy-start.181 = (bf16[3072]{0:T(1024)(128)(2,1)}, bf16[3072]{0:T(1024)(128)(2,1)S(1)}, u32[]{:S(2)}) copy-start(bf16[3072]{0:T(1024)(128)(2,1)S(1)} %reduce.32) | copy-start | bytes 18436
  104.0 438.4 %copy-start.193 = (bf16[1536]{0:T(1024)(128)(2,1)}, bf16[1536]{0:T(1024)(128)(2,1)S(1)}, u32[]{:S(2)}) copy-start(bf16[1536]{0:T(1024)(128)(2,1)S(1)} %reduce.31) | copy-start | bytes 9220
  118.8 423.7 %copy-start.296 = (bf16[48]{0:T(256)(128)(2,1)}, bf16[48]{0:T(256)(128)(2,1)S(1)}, u32[]{:S(2)}) copy-start(bf16[48]{0:T(256)(128)(2,1)S(1)} %get-tuple-element.5482) | copy-start | bytes 292
  118.8 423.7 %copy-start.302 = (bf16[48]{0:T(256)(128)(2,1)}, bf16[48]{0:T(256)(128)(2,1)S(1)}, u32[]{:S(2)}) copy-start(bf16[48]{0:T(256)(128)(2,1)S(1)} %get-tuple-element.5483) | copy-start | bytes 292
  118.8 674.5 %copy-start.186 = (bf16[3328]{0:T(1024)(128)(2,1)}, bf16[3328]{0:T(1024)(128)(2,1)S(1)}, u32[]{:S(2)}) copy-start(bf16[3328]{0:T(1024)(128)(2,1)S(1)} %get-tuple-element.5481) | copy-start | bytes 19972
  146.3 396.2 %copy-start.52 = (bf16[256,1536]{1,0:T(8,128)(2,1)}, bf16[256,1536]{1,0:T(8,128)(2,1)S(1)}, u32[]{:S(2)}) copy-start(bf16[256,1536]{1,0:T(8,128)(2,1)S(1)} %get-tuple-element.5529) | copy-start | bytes 2359300
  654.8 3.4 collective-permute-start
  774.6 4.5 collective-permute-start.1
  826.2 423.3 %collective-permute-start.2 = (bf16[256,1536]{1,0:T(8,128)(2,1)}, bf16[256,1536]{1,0:T(8,128)(2,1)S(1)}, u32[]{:S(2)}, u32[]{:S(2)}) collective-permute-start(bf16[256,1536]{1,0:T(8,128)(2,1)} %get-tuple-element.2930), channel_id=1, source_target_pairs={{16,0},{17,1},{18,2},{19,3},{20,4},{21,5},{22,6},{23,7},{24,8},{25... | collective-permute-start | bytes 2359304 | tf_op jit(solution)/shard_map/ppermute | solution.py:14
  1507.1 39.5 %copy-start.154 = (f32[2,128,48]{2,1,0:T(8,128)S(1)}, f32[2,128,48]{2,1,0:T(8,128)}, u32[]{:S(2)}) copy-start(f32[2,128,48]{2,1,0:T(8,128)} %copy-done.153) | copy-start | bytes 147460 | tf_op jit(solution)/shard_map/cond
  1507.1 40.2 %copy-start.45 = (f32[256,3072]{0,1:T(8,128)S(1)}, f32[256,3072]{0,1:T(8,128)}, u32[]{:S(2)}) copy-start(f32[256,3072]{0,1:T(8,128)} %copy.686) | copy-start | bytes 9437188 | tf_op jit(solution)/shard_map/cond
  1602.1 4.4 collective-permute-start.3
  1864.4 39.6 %copy-start.156 = (f32[2,128,48]{2,1,0:T(8,128)S(1)}, f32[2,128,48]{2,1,0:T(8,128)}, u32[]{:S(2)}) copy-start(f32[2,128,48]{2,1,0:T(8,128)} %copy-done.155) | copy-start | bytes 147460 | tf_op jit(solution)/shard_map/cond
  1864.4 40.3 %copy-start.46 = (f32[256,3072]{0,1:T(8,128)S(1)}, f32[256,3072]{0,1:T(8,128)}, u32[]{:S(2)}) copy-start(f32[256,3072]{0,1:T(8,128)} %copy.715) | copy-start | bytes 9437188 | tf_op jit(solution)/shard_map/cond
  1979.6 489.8 %reduce-scatter.9.cloned.1.call-start = ((), (), s32[]{:S(2)}) async-start(), calls=%async_computation.6 | async-start | bytes 24576000 | tf_op jit(solution)/shard_map/reduce_scatter | solution.py:265
  2023.7 478.8 %reduce-scatter.15.cloned.1.call-start = ((), (), s32[]{:S(2)}) async-start(), calls=%async_computation.9 | async-start | bytes 1064960
  2025.9 494.1 %reduce-scatter.13.cloned.1.call-start = ((), (), s32[]{:S(2)}) async-start(), calls=%async_computation.8 | async-start | bytes 491520
  2028.1 648.8 %all-reduce.67.cloned.1.call-start = ((), (), s32[]{:S(2)}) async-start(), calls=%async_computation.10 | async-start | bytes 14548992 | tf_op jit(solution)/shard_map/psum | solution.py:296
  2502.5 181.5 %copy-start.118 = (bf16[1,2,1,256,1536]{4,3,2,1,0:T(8,128)(2,1)}, bf16[1,2,1,256,1536]{4,3,2,1,0:T(8,128)(2,1)S(1)}, u32[]{:S(2)}) copy-start(bf16[1,2,1,256,1536]{4,3,2,1,0:T(8,128)(2,1)S(1)} %bitcast_dynamic-update-slice_fusion.28) | copy-start | bytes 4718596
  (261 other events, 984.8 us)
Sparse Core Ops, SparseCore 0:
  9.6 196.2 all-gather.4
  207.4 334.9 all-gather.2
  1979.7 159.9 reduce-scatter.10
  2141.9 327.4 reduce-scatter.8
  2472.1 26.1 reduce-scatter.14
  2500.5 19.5 reduce-scatter.12
  2523.7 153.1 all-reduce.66
where the time goes:
time: 2710 us; the launch traced here: 2690 us
  waiting for transfers between devices  1420 us (52%)
  local copies, waits for them, and re-layouts  430 us (16%)
  matrix products  378 us (14%)
  other arithmetic  259 us (10%)
  blocking collectives  167 us (6%)
    ppermute x4, waiting for transfers between devices, from_behind(): lax.ppermute(value, axis, [(source, source + steps) for source in range(f...  429 us
    all_gather x1, waiting for transfers between devices, on_device(): lax.all_gather(shards[0], 'shard', axis=1, tiled=True)  337 us
    reduce_scatter x1, waiting for transfers between devices, on_device(): lax.psum_scatter(total[0].astype(jnp.bfloat16), 'shard', scatter_dimensio...  330 us
    psum x1, waiting for transfers between devices, on_device(): lax.psum(as_sent(owned), 'rep')  133 us
    dot_general x16, matrix products, advance(): jnp.einsum('hij,jhp->ihp', weights * scores[None], x_piece, precision=HIGH)  125 us
    cond x4, local copies, waits for them, and re-layouts, on_device(): lax.cond(active, run_backward, spare_backward, cotangent, block_in, store...  116 us
    reduce_scatter x1, waiting for transfers between devices, on_device(): lax.psum_scatter(total[2].astype(jnp.bfloat16), 'shard', scatter_dimensio...  112 us
    all_gather x1, waiting for transfers between devices, on_device(): lax.all_gather(shards[2], 'shard', axis=1, tiled=True)  59.6 us
  transfers between devices with their start and end apart: 11, of which 10 were waited for; matrix products, arithmetic and copies ran while one was open for 3% of the time, Pallas kernels for 0%

commit v1 on v0

--- a/solution.py
+++ b/solution.py
@@ -6,6 +6,10 @@
 SCAN_BLOCK = 128
 HIGH = lax.Precision.HIGHEST
 EPSILON = 1e-05
+
+
+def serve_rows_on_mesh(mesh_dim, panel):
+    return jnp.concatenate(jax.lax.all_gather(panel, axis_name=mesh_dim), 1)
 
 
 def from_behind(value, axis, steps):
@@ -169,7 +173,7 @@
         out_gain,
     )
     gathered = (
-        lax.all_gather(shards[0], "shard", axis=1, tiled=True),
+        serve_rows_on_mesh("shard", panel=shards[0]),
         lax.all_gather(shards[1], "shard", axis=1, tiled=True),
         lax.all_gather(shards[2], "shard", axis=1, tiled=True),
         lax.all_gather(shards[3], "shard", axis=2, tiled=True),

time: 2710 us -> 2710 us (level)
    all_gather x0 -> x1, waiting for transfers between devices: none -> 336 us  [serve_rows_on_mesh(): return jnp.concatenate(jax.lax.all_gather(panel, axis_name=mesh_dim), 1)]
    all_gather x1, waiting for transfers between devices: 337 us -> 81.5 us  [on_device(): lax.all_gather(shards[0], 'shard', axis=1, tiled=True)]
    ppermute x4, waiting for transfers between devices: 429 us -> 347 us  [from_behind(): lax.ppermute(value, axis, [(source, source + steps) for source in range(f...]
  transfers between devices with their start and end apart: 11 -> 12, of which waited for: 10 -> 11; matrix products, arithmetic and copies ran while one was open for 3% -> 11% of each run, Pallas kernels for 0% -> 0%
where the time goes in v1:
time: 2710 us; the launch traced here: 2700 us
  waiting for transfers between devices  1420 us (52%)
  local copies, waits for them, and re-layouts  433 us (16%)
  matrix products  379 us (14%)
  other arithmetic  259 us (10%)
  blocking collectives  167 us (6%)
    ppermute x4, waiting for transfers between devices, from_behind(): lax.ppermute(value, axis, [(source, source + steps) for source in range(f...  347 us
    all_gather x1, waiting for transfers between devices, serve_rows_on_mesh(): return jnp.concatenate(jax.lax.all_gather(panel, axis_name=mesh_dim), 1)  336 us
    reduce_scatter x1, waiting for transfers between devices, on_device(): lax.psum_scatter(total[0].astype(jnp.bfloat16), 'shard', scatter_dimensio...  330 us
    psum x1, waiting for transfers between devices, on_device(): lax.psum(as_sent(owned), 'rep')  133 us
    dot_general x16, matrix products, advance(): jnp.einsum('hij,jhp->ihp', weights * scores[None], x_piece, precision=HIGH)  125 us
    cond x4, local copies, waits for them, and re-layouts, on_device(): lax.cond(active, run_backward, spare_backward, cotangent, block_in, store...  116 us
    reduce_scatter x1, waiting for transfers between devices, on_device(): lax.psum_scatter(total[2].astype(jnp.bfloat16), 'shard', scatter_dimensio...  111 us
    all_gather x1, waiting for transfers between devices, on_device(): lax.all_gather(shards[0], 'shard', axis=1, tiled=True)  81.5 us
  transfers between devices with their start and end apart: 12, of which 11 were waited for; matrix products, arithmetic and copies ran while one was open for 11% of the time, Pallas kernels for 0%

profile of v1, /device:TPU:0, one launch (start us, length us, event | category | flops | bytes accessed | tf_op | source)
XLA Modules:
  0.0 2697.7 jit_solution(12896643691691952317)
XLA Ops:
  12.6 57.8 %all_gather.46 = bf16[1,4,3328]{1,0,2:T(2,128)(2,1)S(1)} all-gather(bf16[1,4,832]{1,0,2:T(2,128)(2,1)} %copy.733), channel_id=1, replica_groups=mesh['section'=2,'shard'=4,'rep'=4] {'shard'}, dimensions={2}, use_global_device_ids=true | all-gather | bytes 33280 | tf_op jit(solution)/shard_map/all_gather | solution.py:179
  72.3 18.2 all_gather.54
  119.5 25.9 all_gather.50
  146.5 60.0 %all-gather.5.cloned.1.call-done = bf16[1,3072,1536]{2,1,0:T(8,128)(2,1)} async-done(((bf16[1,768,1536]{2,1,0:T(8,128)(2,1)}), bf16[1,3072,1536]{2,1,0:T(8,128)(2,1)}) %all-gather.5.cloned.1.call-update) | async-done | bytes 9437200 | tf_op jit(solution)/shard_map/all_gather | solution.py:178
  206.5 336.4 %all-gather.9.cloned.1.call-done = bf16[4,384,6400]{2,1,0:T(8,128)(2,1)} async-done(((bf16[1,384,6400]{2,1,0:T(8,128)(2,1)}), bf16[4,384,6400]{2,1,0:T(8,128)(2,1)}) %all-gather.9.cloned.1.call-update) | async-done | bytes 19660816 | tf_op jit(solution)/shard_map/all_gather | solution.py:12
  543.0 113.7 %conditional.6 = (bf16[256,1536]{1,0:T(8,128)(2,1)}, bf16[256,1536]{1,0:T(8,128)(2,1)}, f32[256,6400]{1,0:T(8,128)}, f32[256,48]{0,1:T(8,128)}, bf16[256,3072]{1...) conditional(s32[]{:T(128)} %convert_element_type.338, () %tuple.200, (bf16[256,1536]{1,0:T(8,128)(2,1)S(1)}, s32[]{:T(128)}, ...), branch_computations={%region_0.1_spmd, %region_1.7_spmd} | conditional | flops 9355532288 | bytes 165452624 | solution.py:219
  585.3 42.9 %while.240 = (s32[]{:T(128)}, f32[48,64,128]{2,1,0:T(8,128)S(1)}, f32[2,128,48,64]{1,3,2,0:T(8,128)}, f32[2,128,48]{2,1,0:T(8,128)S(1)}, f32[2,128,48,64]{1,0,3,...) while((s32[]{:T(128)}, f32[48,64,128]{2,1,0:T(8,128)S(1)}, ...), condition=%wide.region_5.5_spmd.clone.clone, body=%wide.region_3.4_spmd.clone.clone.sunk | while | flops 1843806208 | bytes 17469076 | solution.py:61
  663.1 113.7 %conditional.7 = (bf16[256,1536]{1,0:T(8,128)(2,1)}, bf16[256,1536]{1,0:T(8,128)(2,1)}, f32[256,6400]{1,0:T(8,128)}, f32[256,48]{0,1:T(8,128)}, bf16[256,3072]{1...) conditional(s32[]{:T(128)} %convert_element_type.339, () %tuple.202, (bf16[256,1536]{1,0:T(8,128)(2,1)S(1)}, s32[]{:T(128)}, ...), branch_computations={%region_7.8_spmd, %region_8.14_spmd} | conditional | flops 9355532288 | bytes 165452624 | solution.py:219
  705.2 43.2 %while.241 = (s32[]{:T(128)}, f32[48,64,128]{2,1,0:T(8,128)S(1)}, f32[2,128,48,64]{1,3,2,0:T(8,128)}, f32[2,128,48]{2,1,0:T(8,128)S(1)}, f32[2,128,48,64]{1,0,3,...) while((s32[]{:T(128)}, f32[48,64,128]{2,1,0:T(8,128)S(1)}, ...), condition=%wide.region_12.12_spmd.clone.clone, body=%wide.region_10.11_spmd.clone.clone.sunk | while | flops 1843806208 | bytes 17469076 | solution.py:61
  797.2 81.5 %all-gather.7.cloned.1.call-done = bf16[1,1536,6400]{2,1,0:T(8,128)(2,1)} async-done(((bf16[1,384,6400]{2,1,0:T(8,128)(2,1)}), bf16[1,1536,6400]{2,1,0:T(8,128)(2,1)}) %all-gather.7.cloned.1.call-update) | async-done | bytes 19660816 | tf_op jit(solution)/shard_map/all_gather | solution.py:227
  879.7 32.9 %conditional.9 = (bf16[256,1536]{1,0:T(8,128)(2,1)}, f32[1536,48]{0,1:T(8,128)}, f32[4,3328]{1,0:T(4,128)}, f32[3328]{0:T(1024)}, f32[48]{0:T(128)}, /*index=5*/...) conditional(s32[]{:T(128)} %convert_element_type.340, ...), branch_computations={%region_21.22_spmd, %region_22.0_spmd} | conditional | flops 20592838656 | bytes 777999360 | solution.py:259
  913.9 339.3 %collective-permute-done.2 = bf16[256,1536]{1,0:T(8,128)(2,1)S(1)} collective-permute-done((bf16[256,1536]{1,0:T(8,128)(2,1)}, bf16[256,1536]{1,0:T(8,128)(2,1)S(1)}, u32[]{:S(2)}, u32[]{:S(2)}) %collective-permute-start.2) | collective-permute-done | bytes 786464 | tf_op jit(solution)/shard_map/ppermute | solution.py:18
  1253.2 353.0 %conditional.10 = (bf16[256,1536]{1,0:T(8,128)(2,1)}, f32[1536,48]{0,1:T(8,128)}, f32[4,3328]{1,0:T(4,128)}, f32[3328]{0:T(1024)}, f32[48]{0:T(128)}, /*index=5*...) conditional(s32[]{:T(128)} %convert_element_type.339, ...), branch_computations={%region_52.54_spmd, %region_53.84_spmd} | conditional | flops 20592838656 | bytes 781147136 | solution.py:259
  1286.9 60.2 %while.245 = (s32[]{:T(128)}, f32[48,64,128]{2,1,0:T(8,128)S(1)}, f32[2,128,48,64]{1,3,2,0:T(8,128)}, f32[2,48,128,128]{3,2,1,0:T(8,128)}, f32[2,128,128]{1,2,0:...) while((s32[]{:T(128)}, f32[48,64,128]{2,1,0:T(8,128)S(1)}, ...), condition=%wide.region_56.57_spmd.clone.clone, body=%wide.region_54.56_spmd.clone.clone.sunk | while | flops 1847734272 | bytes 84601144 | solution.py:61
  1393.8 68.0 %while.246 = (s32[]{:T(128)}, f32[48,64,128]{2,1,0:T(8,128)S(1)}, f32[2,128,48,64]{1,3,2,0:T(8,128)}, f32[2,128,48]{2,1,0:T(8,128)S(1)}, f32[2,128,128]{2,1,0:T(...) while((s32[]{:T(128)}, f32[48,64,128]{2,1,0:T(8,128)S(1)}, ...), condition=%wide.region_68.69_spmd.clone.clone, body=%wide.region_59.68_spmd.clone.clone.sunk | while | flops 3687632896 | bytes 91598432 | solution.py:61
  1493.6 17.5 convolution_bitcast_fusion.3
  1511.0 39.5 %copy.772 = f32[1536,6400]{1,0:T(8,128)} copy(f32[1536,6400]{0,1:T(8,128)} %convolution_bitcast_fusion.3) | data formatting | bytes 78643200 | tf_op jit(solution)/shard_map/cond | solution.py:259
  1587.4 18.8 copy.774
  1610.5 350.8 %conditional.11 = (f32[1536,48]{0,1:T(8,128)}, f32[4,3328]{1,0:T(4,128)}, f32[3328]{0:T(1024)}, f32[48]{0:T(128)}, f32[48]{0:T(128)}, /*index=5*/f32[48]{0:T(128...) conditional(s32[]{:T(128)} %convert_element_type.338, ...), branch_computations={%region_83.85_spmd, %region_84.115_spmd} | conditional | flops 20592838656 | bytes 793205952 | solution.py:259
  1644.2 60.5 %while.247 = (s32[]{:T(128)}, f32[48,64,128]{2,1,0:T(8,128)S(1)}, f32[2,128,48,64]{1,3,2,0:T(8,128)}, f32[2,48,128,128]{3,2,1,0:T(8,128)}, f32[2,128,128]{1,2,0:...) while((s32[]{:T(128)}, f32[48,64,128]{2,1,0:T(8,128)S(1)}, ...), condition=%wide.region_87.88_spmd.clone.clone, body=%wide.region_85.87_spmd.clone.clone.sunk | while | flops 1847734272 | bytes 84601144 | solution.py:61
  1751.6 68.0 %while.248 = (s32[]{:T(128)}, f32[48,64,128]{2,1,0:T(8,128)S(1)}, f32[2,128,48,64]{1,3,2,0:T(8,128)}, f32[2,128,48]{2,1,0:T(8,128)S(1)}, f32[2,128,128]{2,1,0:T(...) while((s32[]{:T(128)}, f32[48,64,128]{2,1,0:T(8,128)S(1)}, ...), condition=%wide.region_99.100_spmd.clone.clone, body=%wide.region_90.99_spmd.clone.clone.sunk | while | flops 3687632896 | bytes 91598432 | solution.py:61
  1851.1 17.4 convolution_bitcast_fusion.6
  1868.5 39.5 %copy.776 = f32[1536,6400]{1,0:T(8,128)} copy(f32[1536,6400]{0,1:T(8,128)} %convolution_bitcast_fusion.6) | data formatting | bytes 78643200 | tf_op jit(solution)/shard_map/cond | solution.py:259
  1942.5 18.6 copy.778
  1961.3 22.4 add_convert_fusion.10
  1983.8 44.0 %add_convert_fusion.9 = bf16[1536,6400]{1,0:T(8,128)(2,1)} fusion(f32[1536,6400]{1,0:T(8,128)} %get-tuple-element.5079, f32[1536,6400]{1,0:T(8,128)} %get-tuple-element.5075, f32[1536,6400]{1,0:T(8,128)} %get-tuple-element.5077), kind=kLoop, calls=%fused_computation.929 | loop fusion | flops 29491200 | bytes 137625600 | tf_op jit(solution)/shard_map/convert_element_type | solution.py:270
  2032.3 111.4 %reduce-scatter.11.cloned.1.call-done = bf16[768,1536]{1,0:T(8,128)(2,1)} async-done(((bf16[3072,1536]{1,0:T(8,128)(2,1)}), bf16[768,1536]{1,0:T(8,128)(2,1)}) %reduce-scatter.11.cloned.1.call-update) | async-done | bytes 2359312 | tf_op jit(solution)/shard_map/reduce_scatter | solution.py:275
  2143.6 329.7 %reduce-scatter.9.cloned.1.call-done = bf16[384,6400]{1,0:T(8,128)(2,1)} async-done(((bf16[1536,6400]{1,0:T(8,128)(2,1)}), bf16[384,6400]{1,0:T(8,128)(2,1)}) %reduce-scatter.9.cloned.1.call-update) | async-done | bytes 4915216 | tf_op jit(solution)/shard_map/reduce_scatter | solution.py:269
  2484.8 19.4 all-reduce.63
  2507.4 16.6 reduce-scatter.13.cloned.1.call-done
  2525.0 18.1 all-reduce.61
  2547.7 133.1 %all-reduce.67.cloned.1.call-done = (bf16[1,384,6400]{2,1,0:T(8,128)(2,1)}, bf16[1,768,1536]{2,1,0:T(8,128)(2,1)}) async-done(((bf16[1,384,6400]{2,1,0:T(8,128)(2,1)}, bf16[1,768,1536]{2,1,0:T(8,128)(2,1)}), (bf16[1,384,6400]{2,1,0:T(8,128)(2,1)}, bf16[1,768,1536]{2,1,0:T(8,128)(2,1)})) %all-reduce.67.cloned.1.call-update) | async-done | bytes 7274512 | tf_op jit(solution)/shard_map/psum | solution.py:300
  (1131 shorter events, 909.8 us)
Async XLA Ops:
  7.2 199.3 %all-gather.5.cloned.1.call-start = ((), (), s32[]{:S(2)}) async-start(), calls=%async_computation.4 | async-start | bytes 11796480 | tf_op jit(solution)/shard_map/all_gather | solution.py:178
  7.9 535.0 %all-gather.9.cloned.1.call-start = ((), (), s32[]{:S(2)}) async-start(), calls=%async_computation.8 | async-start | bytes 24576000 | tf_op jit(solution)/shard_map/all_gather | solution.py:12
  8.7 870.0 %all-gather.7.cloned.1.call-start = ((), (), s32[]{:S(2)}) async-start(), calls=%async_computation.5 | async-start | bytes 24576000 | tf_op jit(solution)/shard_map/all_gather | solution.py:227
  9.4 62.7 %copy-start.252 = (bf16[1,384,48]{1,2,0:T(8,128)(2,1)S(1)}, bf16[1,384,48]{1,2,0:T(8,128)(2,1)}, u32[]{:S(2)}) copy-start(bf16[1,384,48]{1,2,0:T(8,128)(2,1)} %param.46) | copy-start | bytes 110596
  9.4 62.8 %copy-start.276 = (bf16[1,832]{1,0:T(2,128)(2,1)S(1)}, bf16[1,832]{1,0:T(2,128)(2,1)}, u32[]{:S(2)}) copy-start(bf16[1,832]{1,0:T(2,128)(2,1)} %param.49) | copy-start | bytes 4996
  9.4 62.8 %copy-start.277 = (bf16[1,768]{1,0:T(2,128)(2,1)S(1)}, bf16[1,768]{1,0:T(2,128)(2,1)}, u32[]{:S(2)}) copy-start(bf16[1,768]{1,0:T(2,128)(2,1)} %param.54) | copy-start | bytes 4612
  9.5 81.0 %copy-start.291 = (bf16[1,384]{1,0:T(2,128)(2,1)S(1)}, bf16[1,384]{1,0:T(2,128)(2,1)}, u32[]{:S(2)}) copy-start(bf16[1,384]{1,0:T(2,128)(2,1)} %param.53) | copy-start | bytes 2308
  9.5 95.2 %copy-start.292 = (bf16[1,12]{1,0:T(2,128)(2,1)S(1)}, bf16[1,12]{1,0:T(2,128)(2,1)}, u32[]{:S(2)}) copy-start(bf16[1,12]{1,0:T(2,128)(2,1)} %param.51) | copy-start | bytes 76
  9.5 95.5 %copy-start.293 = (bf16[1,12]{1,0:T(2,128)(2,1)S(1)}, bf16[1,12]{1,0:T(2,128)(2,1)}, u32[]{:S(2)}) copy-start(bf16[1,12]{1,0:T(2,128)(2,1)} %param.52) | copy-start | bytes 76
  9.5 95.7 %copy-start.294 = (bf16[1,12]{1,0:T(2,128)(2,1)S(1)}, bf16[1,12]{1,0:T(2,128)(2,1)}, u32[]{:S(2)}) copy-start(bf16[1,12]{1,0:T(2,128)(2,1)} %param.50) | copy-start | bytes 76
  9.5 96.1 %copy-start.275 = (s32[2,1]{0,1:T(1,128)S(1)}, s32[2,1]{0,1:T(1,128)}, u32[]{:S(2)}) copy-start(s32[2,1]{0,1:T(1,128)} %param.44) | copy-start | bytes 28
  9.5 136.0 %copy-start.94 = (bf16[1,2,1,256,1536]{4,3,2,1,0:T(8,128)(2,1)S(1)}, bf16[1,2,1,256,1536]{4,3,2,1,0:T(8,128)(2,1)}, u32[]{:S(2)}) copy-start(bf16[1,2,1,256,1536]{4,3,2,1,0:T(8,128)(2,1)} %param.43) | copy-start | bytes 4718596
  9.5 2134.1 %reduce-scatter.11.cloned.1.call-start = ((), (), s32[]{:S(2)}) async-start(), calls=%async_computation.7 | async-start | bytes 11796480 | tf_op jit(solution)/shard_map/reduce_scatter | solution.py:275
  72.1 470.8 %copy-start.117 = (bf16[1,4,3328]{2,1,0:T(4,128)(2,1)}, bf16[1,4,3328]{2,1,0:T(4,128)(2,1)S(1)}, u32[]{:S(2)}) copy-start(bf16[1,4,3328]{2,1,0:T(4,128)(2,1)S(1)} %copy.734) | copy-start | bytes 79876
  90.5 789.2 %copy-start.178 = (bf16[3072]{0:T(1024)(128)(2,1)}, bf16[3072]{0:T(1024)(128)(2,1)S(1)}, u32[]{:S(2)}) copy-start(bf16[3072]{0:T(1024)(128)(2,1)S(1)} %reduce.32) | copy-start | bytes 18436
  104.6 438.3 %copy-start.192 = (bf16[1536]{0:T(1024)(128)(2,1)}, bf16[1536]{0:T(1024)(128)(2,1)S(1)}, u32[]{:S(2)}) copy-start(bf16[1536]{0:T(1024)(128)(2,1)S(1)} %reduce.31) | copy-start | bytes 9220
  119.5 423.4 %copy-start.295 = (bf16[48]{0:T(256)(128)(2,1)}, bf16[48]{0:T(256)(128)(2,1)S(1)}, u32[]{:S(2)}) copy-start(bf16[48]{0:T(256)(128)(2,1)S(1)} %get-tuple-element.5482) | copy-start | bytes 292
  119.5 423.4 %copy-start.301 = (bf16[48]{0:T(256)(128)(2,1)}, bf16[48]{0:T(256)(128)(2,1)S(1)}, u32[]{:S(2)}) copy-start(bf16[48]{0:T(256)(128)(2,1)S(1)} %get-tuple-element.5483) | copy-start | bytes 292
  119.5 760.2 %copy-start.183 = (bf16[3328]{0:T(1024)(128)(2,1)}, bf16[3328]{0:T(1024)(128)(2,1)S(1)}, u32[]{:S(2)}) copy-start(bf16[3328]{0:T(1024)(128)(2,1)S(1)} %get-tuple-element.5481) | copy-start | bytes 19972
  146.5 396.5 %copy-start.51 = (bf16[256,1536]{1,0:T(8,128)(2,1)}, bf16[256,1536]{1,0:T(8,128)(2,1)S(1)}, u32[]{:S(2)}) copy-start(bf16[256,1536]{1,0:T(8,128)(2,1)S(1)} %get-tuple-element.5529) | copy-start | bytes 2359300
  656.7 3.4 collective-permute-start
  776.8 4.6 collective-permute-start.1
  912.6 340.6 %collective-permute-start.2 = (bf16[256,1536]{1,0:T(8,128)(2,1)}, bf16[256,1536]{1,0:T(8,128)(2,1)S(1)}, u32[]{:S(2)}, u32[]{:S(2)}) collective-permute-start(bf16[256,1536]{1,0:T(8,128)(2,1)} %get-tuple-element.2930), channel_id=1, source_target_pairs={{16,0},{17,1},{18,2},{19,3},{20,4},{21,5},{22,6},{23,7},{24,8},{25... | collective-permute-start | bytes 2359304 | tf_op jit(solution)/shard_map/ppermute | solution.py:18
  1511.0 39.5 %copy-start.151 = (f32[2,128,48]{2,1,0:T(8,128)S(1)}, f32[2,128,48]{2,1,0:T(8,128)}, u32[]{:S(2)}) copy-start(f32[2,128,48]{2,1,0:T(8,128)} %copy-done.150) | copy-start | bytes 147460 | tf_op jit(solution)/shard_map/cond
  1511.0 40.2 %copy-start.43 = (f32[256,3072]{0,1:T(8,128)S(1)}, f32[256,3072]{0,1:T(8,128)}, u32[]{:S(2)}) copy-start(f32[256,3072]{0,1:T(8,128)} %copy.686) | copy-start | bytes 9437188 | tf_op jit(solution)/shard_map/cond
  1606.2 4.4 collective-permute-start.3
  1868.5 40.2 %copy-start.44 = (f32[256,3072]{0,1:T(8,128)S(1)}, f32[256,3072]{0,1:T(8,128)}, u32[]{:S(2)}) copy-start(f32[256,3072]{0,1:T(8,128)} %copy.715) | copy-start | bytes 9437188 | tf_op jit(solution)/shard_map/cond
  1983.7 489.6 %reduce-scatter.9.cloned.1.call-start = ((), (), s32[]{:S(2)}) async-start(), calls=%async_computation.6 | async-start | bytes 24576000 | tf_op jit(solution)/shard_map/reduce_scatter | solution.py:269
  2027.8 478.3 %reduce-scatter.15.cloned.1.call-start = ((), (), s32[]{:S(2)}) async-start(), calls=%async_computation.10 | async-start | bytes 1064960
  2030.0 494.0 %reduce-scatter.13.cloned.1.call-start = ((), (), s32[]{:S(2)}) async-start(), calls=%async_computation.9 | async-start | bytes 491520
  2032.2 648.6 %all-reduce.67.cloned.1.call-start = ((), (), s32[]{:S(2)}) async-start(), calls=%async_computation.11 | async-start | bytes 14548992 | tf_op jit(solution)/shard_map/psum | solution.py:300
  2506.1 181.8 %copy-start.115 = (bf16[1,2,1,256,1536]{4,3,2,1,0:T(8,128)(2,1)}, bf16[1,2,1,256,1536]{4,3,2,1,0:T(8,128)(2,1)S(1)}, u32[]{:S(2)}) copy-start(bf16[1,2,1,256,1536]{4,3,2,1,0:T(8,128)(2,1)S(1)} %bitcast_dynamic-update-slice_fusion.28) | copy-start | bytes 4718596
  (262 other events, 1024.7 us)
Sparse Core Ops, SparseCore 0:
  9.6 196.9 all-gather.4
  208.1 334.8 all-gather.8
  544.5 334.1 all-gather.6
  1983.8 159.7 reduce-scatter.10
  2145.9 327.4 reduce-scatter.8
  2476.1 26.1 reduce-scatter.14
  2504.5 19.4 reduce-scatter.12
  2527.7 153.0 all-reduce.66
